TPU v7x, 512 devices: a whole 4x8x8 slice. The times are simulated.
512 devices in a mesh: wide: 128 (over z, y, core), quad: 4 (over x).
Axes of the slice: x: 4, y: 8, z: 8, core: 2. Of those that a mesh axis runs over, the one named last changes fastest.
Arguments:
- orbitals: float32 [256, 64, 4096], P('wide', 'quad'), may hold values from -6 to 6
- corners: int32 [256, 2], P('wide'), may hold values from 0 to 16
- pair_partner: int32 [512], P('wide'), may hold values from 0 to 255, as said below
- pair_live: int32 [512], P('wide'), may hold values from 0 to 1, as said below
Outputs:
- exchange_action: float32 [256, 64, 4096], P('wide', 'quad')
Inputs may be any that keep to these rules, and one draw needn't show every extreme that they name: For the slots of owner w, the second orbital lies between the first plus 1 and the first plus 4 where the slot is live; every pair_partner is a valid orbital index. The number of live slots differs from owner to owner, and owner 0 has all 4 live. `pair_live`: dead slots may stand anywhere among an owner's slots.
All inputs are finite; a program needn't handle non-finite values.
Results may differ from a plain program's by a relative error of at most 0.0003.
Values sent between devices are 32-bit elements; how exact they have to be, the bound alone decides.
No kernel may reach another device: no remote copies, remote signals or barrier semaphores. Data moves between devices by JAX's collectives and lax.ppermute only.
A program may use at most 64 MiB of HBM per device.

v0:
```python
import functools

import jax
import jax.numpy as jnp
import numpy as np
from jax import lax
from jax.experimental import pallas as pl
from jax.experimental.pallas import tpu as pltpu
from jax.sharding import PartitionSpec as P


BZ = 64
SWEEPS = 8
LANES = 128
ROWS = 16
CHUNKS = 32
PAD = 10
SHELL = 8


def even_coefficients():
    nodes = np.polynomial.chebyshev.Chebyshev.basis(SWEEPS).convert(kind=np.polynomial.Polynomial)
    top = nodes.coef / 6.0 ** np.arange(SWEEPS + 1)
    rest = -top / float(nodes(6.5 / 6.0))
    rest[0] += 1.0
    even = rest[::2]
    g = np.zeros(SWEEPS // 2)
    carry = 0.0
    for k in range(SWEEPS // 2):
        g[k] = (even[k] + carry) / 42.25
        carry = g[k]
    return g


def slot_scalars(slot, place_ref, meta_refs):
    across, own, inside = meta_refs
    first_core = place_ref[1] == 1

    def back(k):
        return jnp.where(first_core, across[k], inside[k])

    right = jnp.clip(back(4 + slot).astype(jnp.int32) - place_ref[0], 0, 5)
    row = right % 2
    step = right // 2
    left = slot % 2

    def offset(dim):
        at = 2 * row + dim
        fore = jnp.where(first_core, inside[at], across[at])
        there = jnp.where(step == 0, back(at), jnp.where(step == 1, own[at], fore))
        return (there - back(2 * left + dim)).astype(jnp.int32)

    which = jnp.where(step < 2, step, jnp.where(first_core, 2, 3))
    return left, row, which, back(8 + slot), offset(0), offset(1)


def shift_parts(shift_y, shift_z, rows):
    shift = shift_y * BZ + shift_z
    whole = shift >> 7
    part = shift & (LANES - 1)
    lane = lax.broadcasted_iota(jnp.int32, (rows, LANES), 1)
    source = (lane & (BZ - 1)) - shift_z
    keep = (source >= 0) & (source < BZ)
    return whole, part, keep & (lane >= part), keep & (lane < part)


def lanes_of(t):
    return pl.ds(t * LANES, LANES)


def lane_table():
    lane = np.arange(LANES)
    half, zpos = lane // BZ, lane % BZ
    along_z = (half[:, None] == half[None, :]) & (np.abs(zpos[:, None] - zpos[None, :]) == 1)
    turned = (half[:, None] != half[None, :]) & (zpos[:, None] == zpos[None, :])
    table = np.concatenate([along_z | turned, turned], axis=1)
    return np.concatenate([table, table], axis=0).astype(np.float32)


FULL = 4 * SHELL


def exchange_kernel(coef, slots, place_ref, across_meta, own_meta, inside_meta, edge_ref,
                    mine_mid, mine_halo, across_mid, across_halo, inside_mid, inside_halo, table_ref,
                    to_across, to_mine, to_inside,
                    back, to_back, rolled, moved_ref, dens, field, parts, sums):
    lower_half = lax.broadcasted_iota(jnp.int32, (FULL, LANES), 1) < BZ
    at_row = lax.broadcasted_iota(jnp.int32, (FULL, LANES), 0)
    inside = jnp.where(at_row < SHELL, edge_ref[0], jnp.where(at_row >= 3 * SHELL, edge_ref[1], 1.0))
    metas = (across_meta, own_meta, inside_meta)
    first_core = place_ref[1]
    low_at = pl.multiple_of(place_ref[2] * SHELL, SHELL)
    high_at = pl.multiple_of((1 - place_ref[2]) * SHELL, SHELL)

    def bands(mid, halo):
        def of(orbital, t):
            return ((0, SHELL, halo[orbital, pl.ds(low_at, SHELL), lanes_of(t)]),
                    (SHELL, 3 * SHELL, mid[orbital, :, lanes_of(t)]),
                    (3 * SHELL, FULL, halo[orbital, pl.ds(high_at, SHELL), lanes_of(t)]))

        return of

    def banded(orbital, t):
        return ((0, FULL, back[orbital, t]),)

    from_inside, from_across = bands(inside_mid, inside_halo), bands(across_mid, across_halo)
    pool = (banded, bands(mine_mid, mine_halo), from_inside, from_across)

    for k, source in enumerate((from_inside, from_across)):
        @pl.when(first_core == k)
        def _():
            for orbital in range(2):
                for t in range(CHUNKS):
                    for lo, hi, value in source(orbital, t):
                        back[orbital, t, lo:hi, :] = value

    for end in (0, PAD + CHUNKS):
        rolled[end : end + PAD] = jnp.zeros((PAD, FULL, LANES), jnp.float32)
    for out in (to_back, to_mine, to_inside, to_across):
        out[...] = jnp.zeros_like(out)

    def cut(slot, t, value):
        high = value.astype(jnp.bfloat16)
        parts[slot, FULL * t : FULL * (t + 1), :LANES] = high
        parts[slot, FULL * t : FULL * (t + 1), LANES:] = (
            value - high.astype(jnp.float32)).astype(jnp.bfloat16)

    def multiply(slot):
        sums[slot, FULL : FULL * (CHUNKS + 1), :] = jnp.dot(
            parts[slot], table_ref[...], preferred_element_type=jnp.float32)

    def turned(slot, t, lo, hi):
        return sums[slot, FULL * (t + 1) + lo : FULL * (t + 1) + hi, LANES:]

    def neighbours(slot, lo, hi):
        before, here = turned(slot, -1, lo, hi), turned(slot, 0, lo, hi)
        at, n = SHELL + lo, hi - lo
        for t in range(CHUNKS):
            after = turned(slot, t + 1, lo, hi)
            total = field[slot, t, at - 1 : at - 1 + n, :] + field[slot, t, at + 1 : at + 1 + n, :]
            total = total + sums[slot, FULL * (t + 1) + lo : FULL * (t + 1) + hi, :LANES]
            yield t, total + jnp.where(lower_half[:n], before, after)
            before, here = here, after

    def sweep(slot, weight):
        for t, total in neighbours(slot, 0, FULL):
            if weight is not None:
                total = total + weight * dens[slot, t]
            total = total * inside
            field[slot, t, SHELL : SHELL + FULL, :] = total
            cut(slot, t, total)
        multiply(slot)

    def pair_density(slot, _):
        left, row, which, live, dy, dz = slot_scalars(slot, place_ref, metas)
        whole, part, first, second = shift_parts(dy, dz, FULL)
        for k, source in enumerate(pool):
            @pl.when(which == k)
            def _():
                for t in range(CHUNKS):
                    for lo, hi, value in source(row, t):
                        rolled[PAD + t, lo:hi, :] = pltpu.roll(value, part, 1)
        for end in (0, FULL * (CHUNKS + 1)):
            sums[slot, end : end + FULL, :] = jnp.zeros((FULL, 2 * LANES), jnp.float32)
        rim = jnp.zeros((SHELL, LANES), jnp.float32)
        for t in range(CHUNKS):
            at = PAD + t - whole
            moved = jnp.where(first, rolled[at], jnp.where(second, rolled[at - 1], 0.0))
            moved_ref[slot, t] = moved[SHELL : SHELL + ROWS]
            field[slot, t, :SHELL, :] = rim
            field[slot, t, SHELL + FULL :, :] = rim
            value = back[left, t] * moved * live
            dens[slot, t] = value
            field[slot, t, SHELL : SHELL + FULL, :] = value
            cut(slot, t, value)
        multiply(slot)
        return 0

    lax.fori_loop(0, slots, pair_density, 0)

    def two_sweeps(k, _):
        weight = jnp.where(k == 0, coef[2] / coef[3], jnp.where(k == 1, coef[1] / coef[3], coef[0] / coef[3]))
        for slot in range(slots):
            sweep(slot, None)
        for slot in range(slots):
            sweep(slot, weight)
        return 0

    lax.fori_loop(0, SWEEPS // 2 - 1, two_sweeps, 0)

    def terms(slot, _):
        left, row, which, _, dy, dz = slot_scalars(slot, place_ref, metas)
        whole, part, first, second = shift_parts(-dy, -dz, ROWS)
        for t, total in neighbours(slot, SHELL, SHELL + ROWS):
            here = field[slot, t, 2 * SHELL : 2 * SHELL + ROWS, :]
            potential = (total + 6.5 * here) * coef[3]
            to_back[left, :, lanes_of(t)] += potential * moved_ref[slot, t]
            rolled[PAD + t, :ROWS, :] = pltpu.roll(
                potential * back[left, t, SHELL : SHELL + ROWS, :], part, 1)
        for k, target in enumerate((to_back, to_mine, to_inside, to_across)):
            @pl.when(which == k)
            def _():
                for t in range(CHUNKS):
                    at = PAD + t - whole
                    target[row, :, lanes_of(t)] += jnp.where(
                        first, rolled[at, :ROWS, :], jnp.where(second, rolled[at - 1, :ROWS, :], 0.0))
        return 0

    lax.fori_loop(0, slots, terms, 0)

    for k, out in enumerate((to_inside, to_across)):
        @pl.when(first_core == k)
        def _():
            out[...] = to_back[...]


def swapped(x, axis, first, ring):
    size = lax.axis_size(axis)
    lower = [i for i in range(first, size, 2) if ring or i + 1 < size]
    pairs = [(i, (i + 1) % size) for i in lower]
    return lax.ppermute(x, axis, pairs + [(b, a) for a, b in pairs])


def across_chips(x):
    return swapped(x, "wide", 1, True)


def inside_chip(x):
    return swapped(x, "wide", 0, True)


def per_device(orbitals, corners, pair_partner, pair_live):
    per_owner, rows, flat = orbitals.shape
    slots = pair_partner.shape[0]
    owners = lax.axis_size("wide")
    owner = lax.axis_index("wide")
    place = lax.axis_index("quad")
    last = lax.axis_size("quad") - 1
    f32 = jnp.float32
    even = 1 - place % 2
    tiles = orbitals.reshape(per_owner, 2, SHELL, flat)
    outer = lax.dynamic_index_in_dim(tiles, even, 1, keepdims=False)
    inner = lax.dynamic_index_in_dim(tiles, 1 - even, 1, keepdims=False)
    meta = jnp.concatenate([corners.reshape(-1), pair_partner, pair_live]).astype(f32)
    halo_one = swapped(outer, "quad", 0, False)
    halo_two = swapped(inner, "quad", 1, False)
    across_meta, inside_meta = across_chips(meta), inside_chip(meta)
    across_mid, inside_mid = across_chips(orbitals), inside_chip(orbitals)
    halo = jnp.concatenate([halo_one, halo_two], axis=1)
    across_halo, inside_halo = across_chips(halo), inside_chip(halo)
    where = jnp.stack([(owner + owners - 1) % owners * per_owner, 1 - owner % 2, even])
    edge = jnp.stack([place > 0, place < last]).astype(f32)

    smem = pl.BlockSpec(memory_space=pltpu.SMEM)
    vmem = pl.BlockSpec(memory_space=pltpu.VMEM)
    box = jax.ShapeDtypeStruct((per_owner, rows, flat), f32)
    to_across, mine, to_inside = pl.pallas_call(
        functools.partial(exchange_kernel, [float(g) for g in even_coefficients()], slots),
        out_shape=(box,) * 3,
        in_specs=[smem] * 5 + [vmem] * 7,
        out_specs=(vmem,) * 3,
        scratch_shapes=[
            pltpu.VMEM((per_owner, CHUNKS, FULL, LANES), f32),
            pltpu.VMEM((per_owner, rows, flat), f32),
            pltpu.VMEM((CHUNKS + 2 * PAD, FULL, LANES), f32),
            pltpu.VMEM((slots, CHUNKS, ROWS, LANES), f32),
            pltpu.VMEM((slots, CHUNKS, FULL, LANES), f32),
            pltpu.VMEM((slots, CHUNKS, FULL + 2 * SHELL, LANES), f32),
            pltpu.VMEM((slots, FULL * CHUNKS, 2 * LANES), jnp.bfloat16),
            pltpu.VMEM((slots, FULL * (CHUNKS + 2), 2 * LANES), f32),
        ],
        compiler_params=pltpu.CompilerParams(vmem_limit_bytes=28 << 20),
        cost_estimate=pl.CostEstimate(flops=60_000_000, bytes_accessed=5 << 20, transcendentals=0),
        name="exchange",
    )(where, across_meta, meta, inside_meta, edge,
      orbitals, halo, across_mid, across_halo, inside_mid, inside_halo,
      jnp.asarray(lane_table(), jnp.bfloat16))
    return mine + across_chips(to_across) + inside_chip(to_inside)


def solution(mesh):
    in_specs = (P("wide", "quad", None), P("wide", None), P("wide"), P("wide"))
    out_specs = P("wide", "quad", None)
    return jax.shard_map(
        per_device, mesh=mesh, in_specs=in_specs, out_specs=out_specs, check_vma=False
    )
```

profile of v0, /device:TPU:4, one launch (start us, length us, event | category | flops | bytes accessed | tf_op | source)
XLA Modules:
  0.0 72.1 jit_solution(4274587168143364232)
XLA Ops:
  0.0 0.0 copy-start
  0.0 1.1 %dynamic-slice_bitcast_fusion = (f32[2,8,4096]{2,1,0:T(8,128)S(1)}, f32[2,8,4096]{2,1,0:T(8,128)S(1)}) fusion(f32[2,2,8,4096]{3,2,1,0:T(8,128)} %bitcast.14, s32[]{:T(128)S(6)} %select_n.26, s32[]{:T(128)S(6)} %select_n.25), kind=kLoop, calls=%fused_computation.1 | loop fusion | bytes 1048584 | tf_op jit(solution)/shard_map/jit(dynamic_index_in_dim)/squeeze | solution.py:243
  1.1 3.1 %collective-permute-start.2 = (f32[2,8,4096]{2,1,0:T(8,128)S(1)}, f32[2,8,4096]{2,1,0:T(8,128)S(1)}, u32[]{:S(2)}, u32[]{:S(2)}) collective-permute-start(f32[2,8,4096]{2,1,0:T(8,128)S(1)} %get-tuple-element.12), channel_id=1, source_target_pairs={{0,1},{2,3},{1,0},{3,2},{4,5},{6,7},{5,4},{7,6},{8,9},{10,11},{9,8... | collective-permute-start | bytes 786440 | tf_op jit(solution)/shard_map/ppermute | solution.py:221
  4.2 0.0 copy-done
  4.3 13.0 %collective-permute-start.4 = (f32[2,16,4096]{2,1,0:T(8,128)S(1)}, f32[2,16,4096]{2,1,0:T(8,128)S(1)}, u32[]{:S(2)}, u32[]{:S(2)}) collective-permute-start(f32[2,16,4096]{2,1,0:T(8,128)S(1)} %copy-done), channel_id=1, source_target_pairs={{4,8},{12,16},{20,24},{28,32},{36,40},{44,48},{52,56},{60,64},{68,... | collective-permute-start | bytes 1572872 | tf_op jit(solution)/shard_map/ppermute | solution.py:221
  17.3 1.9 %collective-permute-start.6 = (f32[2,16,4096]{2,1,0:T(8,128)S(1)}, f32[2,16,4096]{2,1,0:T(8,128)S(1)}, u32[]{:S(2)}, u32[]{:S(2)}) collective-permute-start(f32[2,16,4096]{2,1,0:T(8,128)S(1)} %copy-done), channel_id=1, source_target_pairs={{0,4},{8,12},{16,20},{24,28},{32,36},{40,44},{48,52},{56,60},{64,6... | collective-permute-start | bytes 1572872 | tf_op jit(solution)/shard_map/ppermute | solution.py:221
  19.2 1.9 %collective-permute-start.3 = (f32[2,8,4096]{2,1,0:T(8,128)S(1)}, f32[2,8,4096]{2,1,0:T(8,128)S(1)}, u32[]{:S(2)}, u32[]{:S(2)}) collective-permute-start(f32[2,8,4096]{2,1,0:T(8,128)S(1)} %get-tuple-element.11), channel_id=1, source_target_pairs={{1,2},{2,1},{5,6},{6,5},{9,10},{10,9},{13,14},{14,13},{17,18},{18,... | collective-permute-start | bytes 786440 | tf_op jit(solution)/shard_map/ppermute | solution.py:221
  21.1 0.0 collective-permute-done.2
  21.2 0.0 copy-start.4
  21.2 8.6 %collective-permute-done.3 = f32[2,8,4096]{2,1,0:T(8,128)S(1)} collective-permute-done((f32[2,8,4096]{2,1,0:T(8,128)S(1)}, f32[2,8,4096]{2,1,0:T(8,128)S(1)}, u32[]{:S(2)}, u32[]{:S(2)}) %collective-permute-start.3) | collective-permute-done | bytes 262176 | tf_op jit(solution)/shard_map/ppermute | solution.py:221
  29.8 0.0 copy-start.1
  29.8 0.0 copy-start.2
  29.8 0.0 copy-start.3
  29.9 2.1 %collective-permute-start.7 = (f32[2,16,4096]{2,1,0:T(8,128)S(1)}, f32[2,16,4096]{2,1,0:T(8,128)S(1)}, u32[]{:S(2)}, u32[]{:S(2)}) collective-permute-start(f32[2,16,4096]{2,1,0:T(8,128)S(1)} %constant_dynamic-update-slice_fusion.mine_halo), channel_id=1, source_target_pairs={{0,4},{8,12},{16,20},{24,28},{32,36},{40,44},{48,52},{56,60},{64,6... | collective-permute-start | bytes 1572872 | tf_op jit(solution)/shard_map/ppermute | solution.py:221
  31.9 3.4 %collective-permute-start.5 = (f32[2,16,4096]{2,1,0:T(8,128)S(1)}, f32[2,16,4096]{2,1,0:T(8,128)S(1)}, u32[]{:S(2)}, u32[]{:S(2)}) collective-permute-start(f32[2,16,4096]{2,1,0:T(8,128)S(1)} %constant_dynamic-update-slice_fusion.mine_halo), channel_id=1, source_target_pairs={{4,8},{12,16},{20,24},{28,32},{36,40},{44,48},{52,56},{60,64},{68,... | collective-permute-start | bytes 1572872 | tf_op jit(solution)/shard_map/ppermute | solution.py:221
  35.3 0.0 copy-done.4
  35.3 0.1 reshape.6
  35.4 0.0 copy-done.2
  35.4 0.0 copy-done.3
  35.4 0.1 add_convert_fusion.1.own_meta
  35.5 1.9 %collective-permute-start.1 = (f32[12]{0:T(128)S(1)}, f32[12]{0:T(128)S(1)}, u32[]{:S(2)}, u32[]{:S(2)}) collective-permute-start(f32[12]{0:T(128)S(1)} %add_convert_fusion.1.own_meta), channel_id=1, source_target_pairs={{0,4},{8,12},{16,20},{24,28},{32,36},{40,44},{48,52},{56,60},{64,6... | collective-permute-start | bytes 152 | tf_op jit(solution)/shard_map/ppermute | solution.py:221
  37.4 0.1 add_convert_fusion.edge_ref
  37.5 0.1 pad_add_fusion.place_ref
  37.6 0.9 %collective-permute-done.1.inside_meta = f32[12]{0:T(128)S(1)} collective-permute-done((f32[12]{0:T(128)S(1)}, f32[12]{0:T(128)S(1)}, u32[]{:S(2)}, u32[]{:S(2)}) %collective-permute-start.1) | collective-permute-done | bytes 80 | tf_op jit(solution)/shard_map/ppermute | solution.py:221
  38.5 5.5 %collective-permute-start = (f32[12]{0:T(128)S(1)}, f32[12]{0:T(128)S(1)}, u32[]{:S(2)}, u32[]{:S(2)}) collective-permute-start(f32[12]{0:T(128)S(1)} %add_convert_fusion.1.own_meta), channel_id=1, source_target_pairs={{4,8},{12,16},{20,24},{28,32},{36,40},{44,48},{52,56},{60,64},{68,... | collective-permute-start | bytes 152 | tf_op jit(solution)/shard_map/ppermute | solution.py:221
  44.0 2.7 %collective-permute-done.across_meta = f32[12]{0:T(128)S(1)} collective-permute-done((f32[12]{0:T(128)S(1)}, f32[12]{0:T(128)S(1)}, u32[]{:S(2)}, u32[]{:S(2)}) %collective-permute-start) | collective-permute-done | bytes 80 | tf_op jit(solution)/shard_map/ppermute | solution.py:221
  46.7 0.0 collective-permute-done.4.across_mid
  46.7 0.0 collective-permute-done.6.inside_mid
  46.7 0.0 collective-permute-done.7.inside_halo
  46.7 0.0 collective-permute-done.5.across_halo
  46.7 0.0 copy-done.1
  46.7 10.6 %exchange.1 = (f32[2,16,4096]{2,1,0:T(8,128)S(1)}, f32[2,16,4096]{2,1,0:T(8,128)S(1)}, f32[2,16,4096]{2,1,0:T(8,128)S(1)}) custom-call(s32[3]{0:T(128)S(1)} %pad_add_fusion.place_ref, f32[12]{0:T(128)S(1)} %collective-permute-done.across_meta, f32[12]{0:T(128)S(1)} %add_convert_fusion.1.own_meta, f32[12]{0:T(128)S(1)} %collective-permute-done.1.inside_meta, ...), custom_call_target="tpu_custom_call" | custom-call | flops 60000000 | bytes 5242880 | tf_op jit(solution)/shard_map/exchange/pallas_call | solution.py:257
  57.4 5.6 %collective-permute-start.8 = (f32[2,16,4096]{2,1,0:T(8,128)S(1)}, f32[2,16,4096]{2,1,0:T(8,128)S(1)}, u32[]{:S(2)}, u32[]{:S(2)}) collective-permute-start(f32[2,16,4096]{2,1,0:T(8,128)S(1)} %get-tuple-element.9), channel_id=1, source_target_pairs={{4,8},{12,16},{20,24},{28,32},{36,40},{44,48},{52,56},{60,64},{68,... | collective-permute-start | bytes 1572872 | tf_op jit(solution)/shard_map/ppermute | solution.py:221
  63.0 1.9 %collective-permute-start.9 = (f32[2,16,4096]{2,1,0:T(8,128)S(1)}, f32[2,16,4096]{2,1,0:T(8,128)S(1)}, u32[]{:S(2)}, u32[]{:S(2)}) collective-permute-start(f32[2,16,4096]{2,1,0:T(8,128)S(1)} %get-tuple-element.10), channel_id=1, source_target_pairs={{0,4},{8,12},{16,20},{24,28},{32,36},{40,44},{48,52},{56,60},{64,6... | collective-permute-start | bytes 1572872 | tf_op jit(solution)/shard_map/ppermute | solution.py:221
  64.9 6.3 %collective-permute-done.8 = f32[2,16,4096]{2,1,0:T(8,128)S(1)} collective-permute-done((f32[2,16,4096]{2,1,0:T(8,128)S(1)}, f32[2,16,4096]{2,1,0:T(8,128)S(1)}, u32[]{:S(2)}, u32[]{:S(2)}) %collective-permute-start.8) | collective-permute-done | bytes 524320 | tf_op jit(solution)/shard_map/ppermute | solution.py:221
  71.2 0.0 collective-permute-done.9
  71.2 0.9 %add_add_fusion = f32[2,16,4096]{2,1,0:T(8,128)} fusion(f32[2,16,4096]{2,1,0:T(8,128)S(1)} %collective-permute-done.9, f32[2,16,4096]{2,1,0:T(8,128)S(1)} %get-tuple-element.8, f32[2,16,4096]{2,1,0:T(8,128)S(1)} %collective-permute-done.8), kind=kLoop, calls=%fused_computation | loop fusion | flops 262144 | bytes 2097152 | tf_op jit(solution)/shard_map/add | solution.py:278
  (2 shorter events, 0.0 us)
Async XLA Ops:
  0.0 4.2 %copy-start = (f32[2,16,4096]{2,1,0:T(8,128)S(1)}, f32[2,16,4096]{2,1,0:T(8,128)}, u32[]{:S(2)}) copy-start(f32[2,16,4096]{2,1,0:T(8,128)} %mine_mid.1) | copy-start | bytes 1572868
  1.1 20.0 %collective-permute-start.2 = (f32[2,8,4096]{2,1,0:T(8,128)S(1)}, f32[2,8,4096]{2,1,0:T(8,128)S(1)}, u32[]{:S(2)}, u32[]{:S(2)}) collective-permute-start(f32[2,8,4096]{2,1,0:T(8,128)S(1)} %get-tuple-element.12), channel_id=1, source_target_pairs={{0,1},{2,3},{1,0},{3,2},{4,5},{6,7},{5,4},{7,6},{8,9},{10,11},{9,8... | collective-permute-start | bytes 786440 | tf_op jit(solution)/shard_map/ppermute | solution.py:221
  4.3 42.4 %collective-permute-start.4 = (f32[2,16,4096]{2,1,0:T(8,128)S(1)}, f32[2,16,4096]{2,1,0:T(8,128)S(1)}, u32[]{:S(2)}, u32[]{:S(2)}) collective-permute-start(f32[2,16,4096]{2,1,0:T(8,128)S(1)} %copy-done), channel_id=1, source_target_pairs={{4,8},{12,16},{20,24},{28,32},{36,40},{44,48},{52,56},{60,64},{68,... | collective-permute-start | bytes 1572872 | tf_op jit(solution)/shard_map/ppermute | solution.py:221
  17.3 29.4 %collective-permute-start.6 = (f32[2,16,4096]{2,1,0:T(8,128)S(1)}, f32[2,16,4096]{2,1,0:T(8,128)S(1)}, u32[]{:S(2)}, u32[]{:S(2)}) collective-permute-start(f32[2,16,4096]{2,1,0:T(8,128)S(1)} %copy-done), channel_id=1, source_target_pairs={{0,4},{8,12},{16,20},{24,28},{32,36},{40,44},{48,52},{56,60},{64,6... | collective-permute-start | bytes 1572872 | tf_op jit(solution)/shard_map/ppermute | solution.py:221
  19.2 10.6 %collective-permute-start.3 = (f32[2,8,4096]{2,1,0:T(8,128)S(1)}, f32[2,8,4096]{2,1,0:T(8,128)S(1)}, u32[]{:S(2)}, u32[]{:S(2)}) collective-permute-start(f32[2,8,4096]{2,1,0:T(8,128)S(1)} %get-tuple-element.11), channel_id=1, source_target_pairs={{1,2},{2,1},{5,6},{6,5},{9,10},{10,9},{13,14},{14,13},{17,18},{18,... | collective-permute-start | bytes 786440 | tf_op jit(solution)/shard_map/ppermute | solution.py:221
  21.2 14.1 %copy-start.4 = (s32[2,2]{1,0:T(2,128)S(1)}, s32[2,2]{1,0:T(2,128)}, u32[]{:S(2)}) copy-start(s32[2,2]{1,0:T(2,128)} %param.6) | copy-start | bytes 52
  29.8 16.9 %copy-start.1 = (bf16[256,256]{1,0:T(8,128)(2,1)S(1)}, bf16[256,256]{1,0:T(8,128)(2,1)}, u32[]{:S(2)}) copy-start(bf16[256,256]{1,0:T(8,128)(2,1)} %constant.51.clone.table_ref) | copy-start | bytes 393220
  29.8 5.5 %copy-start.2 = (s32[4]{0:T(128)S(1)}, s32[4]{0:T(128)}, u32[]{:S(2)}) copy-start(s32[4]{0:T(128)} %param.8) | copy-start | bytes 52
  29.8 5.5 %copy-start.3 = (s32[4]{0:T(128)S(1)}, s32[4]{0:T(128)}, u32[]{:S(2)}) copy-start(s32[4]{0:T(128)} %param.7) | copy-start | bytes 52
  29.9 16.9 %collective-permute-start.7 = (f32[2,16,4096]{2,1,0:T(8,128)S(1)}, f32[2,16,4096]{2,1,0:T(8,128)S(1)}, u32[]{:S(2)}, u32[]{:S(2)}) collective-permute-start(f32[2,16,4096]{2,1,0:T(8,128)S(1)} %constant_dynamic-update-slice_fusion.mine_halo), channel_id=1, source_target_pairs={{0,4},{8,12},{16,20},{24,28},{32,36},{40,44},{48,52},{56,60},{64,6... | collective-permute-start | bytes 1572872 | tf_op jit(solution)/shard_map/ppermute | solution.py:221
  31.9 14.8 %collective-permute-start.5 = (f32[2,16,4096]{2,1,0:T(8,128)S(1)}, f32[2,16,4096]{2,1,0:T(8,128)S(1)}, u32[]{:S(2)}, u32[]{:S(2)}) collective-permute-start(f32[2,16,4096]{2,1,0:T(8,128)S(1)} %constant_dynamic-update-slice_fusion.mine_halo), channel_id=1, source_target_pairs={{4,8},{12,16},{20,24},{28,32},{36,40},{44,48},{52,56},{60,64},{68,... | collective-permute-start | bytes 1572872 | tf_op jit(solution)/shard_map/ppermute | solution.py:221
  35.5 3.0 %collective-permute-start.1 = (f32[12]{0:T(128)S(1)}, f32[12]{0:T(128)S(1)}, u32[]{:S(2)}, u32[]{:S(2)}) collective-permute-start(f32[12]{0:T(128)S(1)} %add_convert_fusion.1.own_meta), channel_id=1, source_target_pairs={{0,4},{8,12},{16,20},{24,28},{32,36},{40,44},{48,52},{56,60},{64,6... | collective-permute-start | bytes 152 | tf_op jit(solution)/shard_map/ppermute | solution.py:221
  38.5 8.2 %collective-permute-start = (f32[12]{0:T(128)S(1)}, f32[12]{0:T(128)S(1)}, u32[]{:S(2)}, u32[]{:S(2)}) collective-permute-start(f32[12]{0:T(128)S(1)} %add_convert_fusion.1.own_meta), channel_id=1, source_target_pairs={{4,8},{12,16},{20,24},{28,32},{36,40},{44,48},{52,56},{60,64},{68,... | collective-permute-start | bytes 152 | tf_op jit(solution)/shard_map/ppermute | solution.py:221
  57.4 13.8 %collective-permute-start.8 = (f32[2,16,4096]{2,1,0:T(8,128)S(1)}, f32[2,16,4096]{2,1,0:T(8,128)S(1)}, u32[]{:S(2)}, u32[]{:S(2)}) collective-permute-start(f32[2,16,4096]{2,1,0:T(8,128)S(1)} %get-tuple-element.9), channel_id=1, source_target_pairs={{4,8},{12,16},{20,24},{28,32},{36,40},{44,48},{52,56},{60,64},{68,... | collective-permute-start | bytes 1572872 | tf_op jit(solution)/shard_map/ppermute | solution.py:221
  63.0 8.3 %collective-permute-start.9 = (f32[2,16,4096]{2,1,0:T(8,128)S(1)}, f32[2,16,4096]{2,1,0:T(8,128)S(1)}, u32[]{:S(2)}, u32[]{:S(2)}) collective-permute-start(f32[2,16,4096]{2,1,0:T(8,128)S(1)} %get-tuple-element.10), channel_id=1, source_target_pairs={{0,4},{8,12},{16,20},{24,28},{32,36},{40,44},{48,52},{56,60},{64,6... | collective-permute-start | bytes 1572872 | tf_op jit(solution)/shard_map/ppermute | solution.py:221
where the time goes:
time: 72.5 us; the launch traced here: 72.1 us
  starting transfers between devices  40.3 us (56%)
  waiting for transfers between devices  18.6 us (26%)
  Pallas kernels  10.6 us (15%)
  local copies, waits for them, and re-layouts  1.27 us (2%)
  other arithmetic  1.11 us (2%)
    ppermute x10, starting transfers between devices, swapped(): return lax.ppermute(x, axis, pairs + [(b, a) for a, b in pairs])  40.3 us
    ppermute x10, waiting for transfers between devices, swapped(): return lax.ppermute(x, axis, pairs + [(b, a) for a, b in pairs])  18.6 us
    pallas_call x1, Pallas kernels, per_device(): pl.pallas_call(functools.partial(exchange_kernel, [float(g) for g in even...  10.6 us
  transfers between devices with their start and end apart: 10, of which 4 were waited for; matrix products, arithmetic and copies ran while one was open for 0% of the time, Pallas kernels for 0%

commit v1 on v0

--- a/solution.py
+++ b/solution.py
@@ -81,7 +81,7 @@
 
 
 def exchange_kernel(coef, slots, place_ref, across_meta, own_meta, inside_meta, edge_ref,
-                    mine_mid, mine_halo, across_mid, across_halo, inside_mid, inside_halo, table_ref,
+                    mine_all, across_mid, across_halo, inside_all, table_ref,
                     to_across, to_mine, to_inside,
                     back, to_back, rolled, moved_ref, dens, field, parts, sums):
     lower_half = lax.broadcasted_iota(jnp.int32, (FULL, LANES), 1) < BZ
@@ -89,13 +89,15 @@
     inside = jnp.where(at_row < SHELL, edge_ref[0], jnp.where(at_row >= 3 * SHELL, edge_ref[1], 1.0))
     metas = (across_meta, own_meta, inside_meta)
     first_core = place_ref[1]
-    low_at = pl.multiple_of(place_ref[2] * SHELL, SHELL)
-    high_at = pl.multiple_of((1 - place_ref[2]) * SHELL, SHELL)
-
-    def bands(mid, halo):
+    even = place_ref[2]
+
+    def bands(mid, mid_at, halo, apart):
+        low_at = pl.multiple_of(even * apart, SHELL)
+        high_at = pl.multiple_of((1 - even) * apart, SHELL)
+
         def of(orbital, t):
             return ((0, SHELL, halo[orbital, pl.ds(low_at, SHELL), lanes_of(t)]),
-                    (SHELL, 3 * SHELL, mid[orbital, :, lanes_of(t)]),
+                    (SHELL, 3 * SHELL, mid[orbital, mid_at : mid_at + ROWS, lanes_of(t)]),
                     (3 * SHELL, FULL, halo[orbital, pl.ds(high_at, SHELL), lanes_of(t)]))
 
         return of
@@ -103,8 +105,9 @@
     def banded(orbital, t):
         return ((0, FULL, back[orbital, t]),)
 
-    from_inside, from_across = bands(inside_mid, inside_halo), bands(across_mid, across_halo)
-    pool = (banded, bands(mine_mid, mine_halo), from_inside, from_across)
+    from_inside = bands(inside_all, SHELL, inside_all, 3 * SHELL)
+    from_across = bands(across_mid, 0, across_halo, SHELL)
+    pool = (banded, bands(mine_all, SHELL, mine_all, 3 * SHELL), from_inside, from_across)
 
     for k, source in enumerate((from_inside, from_across)):
         @pl.when(first_core == k)
@@ -242,12 +245,19 @@
     outer = lax.dynamic_index_in_dim(tiles, even, 1, keepdims=False)
     inner = lax.dynamic_index_in_dim(tiles, 1 - even, 1, keepdims=False)
     meta = jnp.concatenate([corners.reshape(-1), pair_partner, pair_live]).astype(f32)
+    unused = (SHELL - 1) * (1 - even)
+    outer = lax.dynamic_update_slice(outer, meta.reshape(1, 1, -1), (0, unused, 0))
     halo_one = swapped(outer, "quad", 0, False)
     halo_two = swapped(inner, "quad", 1, False)
-    across_meta, inside_meta = across_chips(meta), inside_chip(meta)
-    across_mid, inside_mid = across_chips(orbitals), inside_chip(orbitals)
-    halo = jnp.concatenate([halo_one, halo_two], axis=1)
-    across_halo, inside_halo = across_chips(halo), inside_chip(halo)
+    across_mid = across_chips(orbitals)
+    across_halo = across_chips(jnp.concatenate([halo_one, halo_two], axis=1))
+    mine_all = jnp.concatenate([halo_one, orbitals, halo_two], axis=1)
+    inside_all = inside_chip(mine_all)
+
+    def meta_of(halos):
+        return lax.dynamic_slice(halos, (0, SHELL - 1 - unused, 0), (1, 1, meta.size)).reshape(-1)
+
+    across_meta, inside_meta = meta_of(across_halo), meta_of(inside_all)
     where = jnp.stack([(owner + owners - 1) % owners * per_owner, 1 - owner % 2, even])
     edge = jnp.stack([place > 0, place < last]).astype(f32)
 
@@ -257,7 +267,7 @@
     to_across, mine, to_inside = pl.pallas_call(
         functools.partial(exchange_kernel, [float(g) for g in even_coefficients()], slots),
         out_shape=(box,) * 3,
-        in_specs=[smem] * 5 + [vmem] * 7,
+        in_specs=[smem] * 5 + [vmem] * 5,
         out_specs=(vmem,) * 3,
         scratch_shapes=[
             pltpu.VMEM((per_owner, CHUNKS, FULL, LANES), f32),
@@ -273,7 +283,7 @@
         cost_estimate=pl.CostEstimate(flops=60_000_000, bytes_accessed=5 << 20, transcendentals=0),
         name="exchange",
     )(where, across_meta, meta, inside_meta, edge,
-      orbitals, halo, across_mid, across_halo, inside_mid, inside_halo,
+      mine_all, across_mid, across_halo, inside_all,
       jnp.asarray(lane_table(), jnp.bfloat16))
     return mine + across_chips(to_across) + inside_chip(to_inside)
 

time: 72.5 us -> 72.1 us (level)
  starting transfers between devices: 40.3 us -> 33.8 us
  local copies, waits for them, and re-layouts: 1.27 us -> 3.95 us
  waiting for transfers between devices: 18.6 us -> 21.2 us
  other arithmetic: 1.11 us -> 2.01 us
    ppermute x10 -> x7, starting transfers between devices: 40.3 us -> 33.8 us  [swapped(): return lax.ppermute(x, axis, pairs + [(b, a) for a, b in pairs])]
    ppermute x10 -> x7, waiting for transfers between devices: 18.6 us -> 21.2 us  [swapped(): return lax.ppermute(x, axis, pairs + [(b, a) for a, b in pairs])]
    unnamed x11 -> x10, local copies, waits for them, and re-layouts: 0.05 us -> 2.45 us
    concatenate x0 -> x1, other arithmetic: none -> 0.83 us  [per_device(): across_halo = across_chips(jnp.concatenate([halo_one, halo_two], axis=1))]
  transfers between devices with their start and end apart: 10 -> 7, of which waited for: 4 -> 4; matrix products, arithmetic and copies ran while one was open for 0% -> 3% of each run, Pallas kernels for 0% -> 0%
where the time goes in v1:
time: 72.1 us; the launch traced here: 71.7 us
  starting transfers between devices  33.8 us (47%)
  waiting for transfers between devices  21.2 us (29%)
  Pallas kernels  10.6 us (15%)
  local copies, waits for them, and re-layouts  3.95 us (5%)
  other arithmetic  2.01 us (3%)
    ppermute x7, starting transfers between devices, swapped(): return lax.ppermute(x, axis, pairs + [(b, a) for a, b in pairs])  33.8 us
    ppermute x7, waiting for transfers between devices, swapped(): return lax.ppermute(x, axis, pairs + [(b, a) for a, b in pairs])  21.2 us
    pallas_call x1, Pallas kernels, per_device(): pl.pallas_call(functools.partial(exchange_kernel, [float(g) for g in even...  10.6 us
    unnamed x10, local copies, waits for them, and re-layouts  2.45 us
  transfers between devices with their start and end apart: 7, of which 4 were waited for; matrix products, arithmetic and copies ran while one was open for 3% of the time, Pallas kernels for 0%

profile of v1, /device:TPU:4, one launch (start us, length us, event | category | flops | bytes accessed | tf_op | source)
XLA Modules:
  0.0 71.7 jit_solution(2483911029170377863)
XLA Ops:
  0.0 0.0 copy-start.3
  0.0 0.7 copy-done.3
  0.7 0.1 concatenate.24
  0.8 0.0 copy-start.1
  0.8 0.0 copy-start.2
  0.8 0.7 copy-done.1
  1.4 0.0 copy-done.2
  1.4 0.1 add_convert_fusion.1
  1.5 1.1 %dynamic-slice_bitcast_fusion.1 = (f32[2,8,4096]{2,1,0:T(8,128)S(1)}, f32[2,8,4096]{2,1,0:T(8,128)S(1)}) fusion(f32[2,2,8,4096]{3,2,1,0:T(8,128)} %bitcast.3, s32[]{:T(128)S(6)} %select_n.34, s32[]{:T(128)S(6)} %select_n.36), kind=kLoop, calls=%fused_computation.3 | loop fusion | bytes 1048584 | tf_op jit(solution)/shard_map/jit(dynamic_index_in_dim)/squeeze | solution.py:245
  2.6 0.2 dynamic_update_slice.3
  2.8 3.1 %collective-permute-start = (f32[2,8,4096]{2,1,0:T(8,128)S(1)}, f32[2,8,4096]{2,1,0:T(8,128)S(1)}, u32[]{:S(2)}, u32[]{:S(2)}) collective-permute-start(f32[2,8,4096]{2,1,0:T(8,128)S(1)} %dynamic_update_slice.3), channel_id=1, source_target_pairs={{0,1},{2,3},{1,0},{3,2},{4,5},{6,7},{5,4},{7,6},{8,9},{10,11},{9,8... | collective-permute-start | bytes 786440 | tf_op jit(solution)/shard_map/ppermute | solution.py:224
  5.9 7.1 %collective-permute-start.1 = (f32[2,8,4096]{2,1,0:T(8,128)S(1)}, f32[2,8,4096]{2,1,0:T(8,128)S(1)}, u32[]{:S(2)}, u32[]{:S(2)}) collective-permute-start(f32[2,8,4096]{2,1,0:T(8,128)S(1)} %get-tuple-element.12), channel_id=1, source_target_pairs={{1,2},{2,1},{5,6},{6,5},{9,10},{10,9},{13,14},{14,13},{17,18},{18,... | collective-permute-start | bytes 786440 | tf_op jit(solution)/shard_map/ppermute | solution.py:224
  13.1 0.0 collective-permute-done
  13.1 1.1 %constant_dynamic-update-slice_fusion.1 = f32[2,32,4096]{2,1,0:T(8,128)S(1)} fusion(f32[2,32,4096]{2,1,0:T(8,128)S(1)} %constant_dynamic-update-slice_fusion.2, f32[2,16,4096]{2,1,0:T(8,128)} %param.5), kind=kLoop, calls=%fused_computation.5 | loop fusion | bytes 1048576
  14.2 3.2 %collective-permute-done.1 = f32[2,8,4096]{2,1,0:T(8,128)S(1)} collective-permute-done((f32[2,8,4096]{2,1,0:T(8,128)S(1)}, f32[2,8,4096]{2,1,0:T(8,128)S(1)}, u32[]{:S(2)}, u32[]{:S(2)}) %collective-permute-start.1) | collective-permute-done | bytes 262176 | tf_op jit(solution)/shard_map/ppermute | solution.py:224
  17.4 1.9 %collective-permute-start.3 = (f32[2,32,4096]{2,1,0:T(8,128)S(1)}, f32[2,32,4096]{2,1,0:T(8,128)S(1)}, u32[]{:S(2)}, u32[]{:S(2)}) collective-permute-start(f32[2,32,4096]{2,1,0:T(8,128)S(1)} %constant_dynamic-update-slice_fusion.mine_all), channel_id=1, source_target_pairs={{0,4},{8,12},{16,20},{24,28},{32,36},{40,44},{48,52},{56,60},{64,6... | collective-permute-start | bytes 3145736 | tf_op jit(solution)/shard_map/ppermute | solution.py:224
  19.4 0.0 copy-start
  19.4 0.8 %pad_maximum_fusion = f32[2,16,4096]{2,1,0:T(8,128)} fusion(f32[2,8,4096]{2,1,0:T(8,128)S(1)} %collective-permute-done.1, f32[2,8,4096]{2,1,0:T(8,128)S(1)} %collective-permute-done), kind=kLoop, calls=%fused_computation | loop fusion | flops 131072 | bytes 1048576 | tf_op jit(solution)/shard_map/concatenate | solution.py:253
  20.2 12.1 %collective-permute-start.2 = (f32[2,16,4096]{2,1,0:T(8,128)}, f32[2,16,4096]{2,1,0:T(8,128)S(1)}, u32[]{:S(2)}, u32[]{:S(2)}) collective-permute-start(f32[2,16,4096]{2,1,0:T(8,128)} %pad_maximum_fusion), channel_id=1, source_target_pairs={{4,8},{12,16},{20,24},{28,32},{36,40},{44,48},{52,56},{60,64},{68,... | collective-permute-start | bytes 1572872 | tf_op jit(solution)/shard_map/ppermute | solution.py:224
  32.3 1.9 %collective-permute-start.4 = (f32[2,16,4096]{2,1,0:T(8,128)}, f32[2,16,4096]{2,1,0:T(8,128)S(1)}, u32[]{:S(2)}, u32[]{:S(2)}) collective-permute-start(f32[2,16,4096]{2,1,0:T(8,128)} %param.5), channel_id=1, source_target_pairs={{4,8},{12,16},{20,24},{28,32},{36,40},{44,48},{52,56},{60,64},{68,... | collective-permute-start | bytes 1572872 | tf_op jit(solution)/shard_map/ppermute | solution.py:224
  34.3 0.1 reshape.58
  34.4 0.1 add_convert_fusion.2.own_meta
  34.5 0.1 add_convert_fusion.edge_ref
  34.5 0.1 pad_add_fusion.place_ref
  34.6 4.8 %collective-permute-done.2.across_halo = f32[2,16,4096]{2,1,0:T(8,128)S(1)} collective-permute-done((f32[2,16,4096]{2,1,0:T(8,128)}, f32[2,16,4096]{2,1,0:T(8,128)S(1)}, u32[]{:S(2)}, u32[]{:S(2)}) %collective-permute-start.2) | collective-permute-done | bytes 524320 | tf_op jit(solution)/shard_map/ppermute | solution.py:224
  39.4 0.0 collective-permute-done.3.inside_all
  39.4 6.9 %collective-permute-done.4.across_mid = f32[2,16,4096]{2,1,0:T(8,128)S(1)} collective-permute-done((f32[2,16,4096]{2,1,0:T(8,128)}, f32[2,16,4096]{2,1,0:T(8,128)S(1)}, u32[]{:S(2)}, u32[]{:S(2)}) %collective-permute-start.4) | collective-permute-done | bytes 524320 | tf_op jit(solution)/shard_map/ppermute | solution.py:224
  46.4 0.0 copy-done
  46.4 10.6 %exchange.1 = (f32[2,16,4096]{2,1,0:T(8,128)S(1)}, f32[2,16,4096]{2,1,0:T(8,128)S(1)}, f32[2,16,4096]{2,1,0:T(8,128)S(1)}) custom-call(s32[3]{0:T(128)S(1)} %pad_add_fusion.place_ref, f32[12]{0:T(128)S(1)} %fusion.across_meta, f32[12]{0:T(128)S(1)} %add_convert_fusion.2.own_meta, f32[12]{0:T(128)S(1)} %fusion.1.inside_meta, f32[2]{0:T(128)S(1)} %add_convert_fusion.edge_ref, ...), custom_call_target="tpu_custom_call" | custom-call | flops 60000000 | bytes 5242880 | tf_op jit(solution)/shard_map/exchange/pallas_call | solution.py:267
  57.0 5.6 %collective-permute-start.5 = (f32[2,16,4096]{2,1,0:T(8,128)S(1)}, f32[2,16,4096]{2,1,0:T(8,128)S(1)}, u32[]{:S(2)}, u32[]{:S(2)}) collective-permute-start(f32[2,16,4096]{2,1,0:T(8,128)S(1)} %get-tuple-element.9), channel_id=1, source_target_pairs={{4,8},{12,16},{20,24},{28,32},{36,40},{44,48},{52,56},{60,64},{68,... | collective-permute-start | bytes 1572872 | tf_op jit(solution)/shard_map/ppermute | solution.py:224
  62.7 1.9 %collective-permute-start.6 = (f32[2,16,4096]{2,1,0:T(8,128)S(1)}, f32[2,16,4096]{2,1,0:T(8,128)S(1)}, u32[]{:S(2)}, u32[]{:S(2)}) collective-permute-start(f32[2,16,4096]{2,1,0:T(8,128)S(1)} %get-tuple-element.10), channel_id=1, source_target_pairs={{0,4},{8,12},{16,20},{24,28},{32,36},{40,44},{48,52},{56,60},{64,6... | collective-permute-start | bytes 1572872 | tf_op jit(solution)/shard_map/ppermute | solution.py:224
  64.6 6.2 %collective-permute-done.5 = f32[2,16,4096]{2,1,0:T(8,128)S(1)} collective-permute-done((f32[2,16,4096]{2,1,0:T(8,128)S(1)}, f32[2,16,4096]{2,1,0:T(8,128)S(1)}, u32[]{:S(2)}, u32[]{:S(2)}) %collective-permute-start.5) | collective-permute-done | bytes 524320 | tf_op jit(solution)/shard_map/ppermute | solution.py:224
  70.8 0.0 collective-permute-done.6
  70.8 0.9 %add_add_fusion = f32[2,16,4096]{2,1,0:T(8,128)} fusion(f32[2,16,4096]{2,1,0:T(8,128)S(1)} %collective-permute-done.6, f32[2,16,4096]{2,1,0:T(8,128)S(1)} %get-tuple-element.8, f32[2,16,4096]{2,1,0:T(8,128)S(1)} %collective-permute-done.5), kind=kLoop, calls=%fused_computation.1 | loop fusion | flops 262144 | bytes 2097152 | tf_op jit(solution)/shard_map/add | solution.py:288
  (4 shorter events, 0.1 us)
Async XLA Ops:
  0.0 0.7 copy-start.3
  0.8 0.7 copy-start.1
  0.8 0.7 copy-start.2
  2.8 10.2 %collective-permute-start = (f32[2,8,4096]{2,1,0:T(8,128)S(1)}, f32[2,8,4096]{2,1,0:T(8,128)S(1)}, u32[]{:S(2)}, u32[]{:S(2)}) collective-permute-start(f32[2,8,4096]{2,1,0:T(8,128)S(1)} %dynamic_update_slice.3), channel_id=1, source_target_pairs={{0,1},{2,3},{1,0},{3,2},{4,5},{6,7},{5,4},{7,6},{8,9},{10,11},{9,8... | collective-permute-start | bytes 786440 | tf_op jit(solution)/shard_map/ppermute | solution.py:224
  5.9 11.5 %collective-permute-start.1 = (f32[2,8,4096]{2,1,0:T(8,128)S(1)}, f32[2,8,4096]{2,1,0:T(8,128)S(1)}, u32[]{:S(2)}, u32[]{:S(2)}) collective-permute-start(f32[2,8,4096]{2,1,0:T(8,128)S(1)} %get-tuple-element.12), channel_id=1, source_target_pairs={{1,2},{2,1},{5,6},{6,5},{9,10},{10,9},{13,14},{14,13},{17,18},{18,... | collective-permute-start | bytes 786440 | tf_op jit(solution)/shard_map/ppermute | solution.py:224
  17.4 22.0 %collective-permute-start.3 = (f32[2,32,4096]{2,1,0:T(8,128)S(1)}, f32[2,32,4096]{2,1,0:T(8,128)S(1)}, u32[]{:S(2)}, u32[]{:S(2)}) collective-permute-start(f32[2,32,4096]{2,1,0:T(8,128)S(1)} %constant_dynamic-update-slice_fusion.mine_all), channel_id=1, source_target_pairs={{0,4},{8,12},{16,20},{24,28},{32,36},{40,44},{48,52},{56,60},{64,6... | collective-permute-start | bytes 3145736 | tf_op jit(solution)/shard_map/ppermute | solution.py:224
  19.4 27.0 %copy-start = (bf16[256,256]{1,0:T(8,128)(2,1)S(1)}, bf16[256,256]{1,0:T(8,128)(2,1)}, u32[]{:S(2)}) copy-start(bf16[256,256]{1,0:T(8,128)(2,1)} %constant.61.clone.table_ref) | copy-start | bytes 393220
  20.2 19.2 %collective-permute-start.2 = (f32[2,16,4096]{2,1,0:T(8,128)}, f32[2,16,4096]{2,1,0:T(8,128)S(1)}, u32[]{:S(2)}, u32[]{:S(2)}) collective-permute-start(f32[2,16,4096]{2,1,0:T(8,128)} %pad_maximum_fusion), channel_id=1, source_target_pairs={{4,8},{12,16},{20,24},{28,32},{36,40},{44,48},{52,56},{60,64},{68,... | collective-permute-start | bytes 1572872 | tf_op jit(solution)/shard_map/ppermute | solution.py:224
  32.3 14.0 %collective-permute-start.4 = (f32[2,16,4096]{2,1,0:T(8,128)}, f32[2,16,4096]{2,1,0:T(8,128)S(1)}, u32[]{:S(2)}, u32[]{:S(2)}) collective-permute-start(f32[2,16,4096]{2,1,0:T(8,128)} %param.5), channel_id=1, source_target_pairs={{4,8},{12,16},{20,24},{28,32},{36,40},{44,48},{52,56},{60,64},{68,... | collective-permute-start | bytes 1572872 | tf_op jit(solution)/shard_map/ppermute | solution.py:224
  57.0 13.8 %collective-permute-start.5 = (f32[2,16,4096]{2,1,0:T(8,128)S(1)}, f32[2,16,4096]{2,1,0:T(8,128)S(1)}, u32[]{:S(2)}, u32[]{:S(2)}) collective-permute-start(f32[2,16,4096]{2,1,0:T(8,128)S(1)} %get-tuple-element.9), channel_id=1, source_target_pairs={{4,8},{12,16},{20,24},{28,32},{36,40},{44,48},{52,56},{60,64},{68,... | collective-permute-start | bytes 1572872 | tf_op jit(solution)/shard_map/ppermute | solution.py:224
  62.7 8.2 %collective-permute-start.6 = (f32[2,16,4096]{2,1,0:T(8,128)S(1)}, f32[2,16,4096]{2,1,0:T(8,128)S(1)}, u32[]{:S(2)}, u32[]{:S(2)}) collective-permute-start(f32[2,16,4096]{2,1,0:T(8,128)S(1)} %get-tuple-element.10), channel_id=1, source_target_pairs={{0,4},{8,12},{16,20},{24,28},{32,36},{40,44},{48,52},{56,60},{64,6... | collective-permute-start | bytes 1572872 | tf_op jit(solution)/shard_map/ppermute | solution.py:224

commit v2 on v1

--- a/solution.py
+++ b/solution.py
@@ -81,7 +81,7 @@
 
 
 def exchange_kernel(coef, slots, place_ref, across_meta, own_meta, inside_meta, edge_ref,
-                    mine_all, across_mid, across_halo, inside_all, table_ref,
+                    mine_mid, mine_halo, across_mid, across_halo, inside_all, table_ref,
                     to_across, to_mine, to_inside,
                     back, to_back, rolled, moved_ref, dens, field, parts, sums):
     lower_half = lax.broadcasted_iota(jnp.int32, (FULL, LANES), 1) < BZ
@@ -90,24 +90,29 @@
     metas = (across_meta, own_meta, inside_meta)
     first_core = place_ref[1]
     even = place_ref[2]
-
-    def bands(mid, mid_at, halo, apart):
-        low_at = pl.multiple_of(even * apart, SHELL)
-        high_at = pl.multiple_of((1 - even) * apart, SHELL)
-
+    low_of, high_of = even, 1 - even
+
+    def bands(halo, mid):
         def of(orbital, t):
-            return ((0, SHELL, halo[orbital, pl.ds(low_at, SHELL), lanes_of(t)]),
-                    (SHELL, 3 * SHELL, mid[orbital, mid_at : mid_at + ROWS, lanes_of(t)]),
-                    (3 * SHELL, FULL, halo[orbital, pl.ds(high_at, SHELL), lanes_of(t)]))
+            return ((0, SHELL, halo[low_of, orbital, :, lanes_of(t)]),
+                    *mid(orbital, t),
+                    (3 * SHELL, FULL, halo[high_of, orbital, :, lanes_of(t)]))
 
         return of
+
+    def slab(mid):
+        return lambda orbital, t: ((SHELL, 3 * SHELL, mid[orbital, :, lanes_of(t)]),)
+
+    def last_tiles(orbital, t):
+        return tuple(
+            ((1 + k) * SHELL, (2 + k) * SHELL, inside_all[2 + k, orbital, :, lanes_of(t)]) for k in range(2))
 
     def banded(orbital, t):
         return ((0, FULL, back[orbital, t]),)
 
-    from_inside = bands(inside_all, SHELL, inside_all, 3 * SHELL)
-    from_across = bands(across_mid, 0, across_halo, SHELL)
-    pool = (banded, bands(mine_all, SHELL, mine_all, 3 * SHELL), from_inside, from_across)
+    from_inside = bands(inside_all, last_tiles)
+    from_across = bands(across_halo, slab(across_mid))
+    pool = (banded, bands(mine_halo, slab(mine_mid)), from_inside, from_across)
 
     for k, source in enumerate((from_inside, from_across)):
         @pl.when(first_core == k)
@@ -250,12 +255,14 @@
     halo_one = swapped(outer, "quad", 0, False)
     halo_two = swapped(inner, "quad", 1, False)
     across_mid = across_chips(orbitals)
-    across_halo = across_chips(jnp.concatenate([halo_one, halo_two], axis=1))
-    mine_all = jnp.concatenate([halo_one, orbitals, halo_two], axis=1)
+    halo = jnp.stack([halo_one, halo_two])
+    across_halo = across_chips(halo)
+    mine_all = jnp.concatenate([halo, jnp.moveaxis(tiles, 1, 0)])
     inside_all = inside_chip(mine_all)
 
     def meta_of(halos):
-        return lax.dynamic_slice(halos, (0, SHELL - 1 - unused, 0), (1, 1, meta.size)).reshape(-1)
+        return lax.dynamic_slice(
+            halos, (0, 0, SHELL - 1 - unused, 0), (1, 1, 1, meta.size)).reshape(-1)
 
     across_meta, inside_meta = meta_of(across_halo), meta_of(inside_all)
     where = jnp.stack([(owner + owners - 1) % owners * per_owner, 1 - owner % 2, even])
@@ -267,7 +274,7 @@
     to_across, mine, to_inside = pl.pallas_call(
         functools.partial(exchange_kernel, [float(g) for g in even_coefficients()], slots),
         out_shape=(box,) * 3,
-        in_specs=[smem] * 5 + [vmem] * 5,
+        in_specs=[smem] * 5 + [vmem] * 6,
         out_specs=(vmem,) * 3,
         scratch_shapes=[
             pltpu.VMEM((per_owner, CHUNKS, FULL, LANES), f32),
@@ -283,7 +290,7 @@
         cost_estimate=pl.CostEstimate(flops=60_000_000, bytes_accessed=5 << 20, transcendentals=0),
         name="exchange",
     )(where, across_meta, meta, inside_meta, edge,
-      mine_all, across_mid, across_halo, inside_all,
+      orbitals, halo, across_mid, across_halo, inside_all,
       jnp.asarray(lane_table(), jnp.bfloat16))
     return mine + across_chips(to_across) + inside_chip(to_inside)
 

time: 72.1 us -> 72.1 us (level)
  local copies, waits for them, and re-layouts: 3.95 us -> 2.93 us
  waiting for transfers between devices: 21.2 us -> 22 us
    unnamed x10, local copies, waits for them, and re-layouts: 2.45 us -> 1.36 us
    ppermute x7, waiting for transfers between devices: 21.2 us -> 22 us  [swapped(): return lax.ppermute(x, axis, pairs + [(b, a) for a, b in pairs])]
  transfers between devices with their start and end apart: 7 -> 7, of which waited for: 4 -> 4; matrix products, arithmetic and copies ran while one was open for 3% -> 1% of each run, Pallas kernels for 0% -> 0%
where the time goes in v2:
time: 72.1 us; the launch traced here: 71.8 us
  starting transfers between devices  33.8 us (47%)
  waiting for transfers between devices  22 us (31%)
  Pallas kernels  10.6 us (15%)
  local copies, waits for them, and re-layouts  2.93 us (4%)
  other arithmetic  2.26 us (3%)
    ppermute x7, starting transfers between devices, swapped(): return lax.ppermute(x, axis, pairs + [(b, a) for a, b in pairs])  33.8 us
    ppermute x7, waiting for transfers between devices, swapped(): return lax.ppermute(x, axis, pairs + [(b, a) for a, b in pairs])  22 us
    pallas_call x1, Pallas kernels, per_device(): pl.pallas_call(functools.partial(exchange_kernel, [float(g) for g in even...  10.6 us
  transfers between devices with their start and end apart: 7, of which 4 were waited for; matrix products, arithmetic and copies ran while one was open for 1% of the time, Pallas kernels for 0%

profile of v2, /device:TPU:4, one launch (start us, length us, event | category | flops | bytes accessed | tf_op | source)
XLA Modules:
  0.0 71.8 jit_solution(17337071704511702855)
XLA Ops:
  0.0 0.0 copy-start.4
  0.0 0.7 copy-done.4
  0.7 0.1 concatenate.22
  0.8 0.0 copy-start.2
  0.8 0.0 copy-start.3
  0.8 0.7 copy-done.2
  1.4 0.0 copy-done.3
  1.4 0.1 add_convert_fusion.1
  1.5 0.0 copy-start
  1.5 1.1 %dynamic-slice_bitcast_fusion.1 = (f32[2,8,4096]{2,1,0:T(8,128)S(1)}, f32[2,8,4096]{2,1,0:T(8,128)S(1)}) fusion(f32[2,2,8,4096]{3,2,1,0:T(8,128)} %bitcast.22, s32[]{:T(128)S(6)} %select_n.32, s32[]{:T(128)S(6)} %select_n.34), kind=kLoop, calls=%fused_computation.5 | loop fusion | bytes 1048584 | tf_op jit(solution)/shard_map/jit(dynamic_index_in_dim)/squeeze | solution.py:250
  2.6 0.2 dynamic_update_slice.3
  2.9 3.1 %collective-permute-start = (f32[2,8,4096]{2,1,0:T(8,128)S(1)}, f32[2,8,4096]{2,1,0:T(8,128)S(1)}, u32[]{:S(2)}, u32[]{:S(2)}) collective-permute-start(f32[2,8,4096]{2,1,0:T(8,128)S(1)} %dynamic_update_slice.3), channel_id=1, source_target_pairs={{0,1},{2,3},{1,0},{3,2},{4,5},{6,7},{5,4},{7,6},{8,9},{10,11},{9,8... | collective-permute-start | bytes 786440 | tf_op jit(solution)/shard_map/ppermute | solution.py:229
  6.0 7.1 %collective-permute-start.1 = (f32[2,8,4096]{2,1,0:T(8,128)S(1)}, f32[2,8,4096]{2,1,0:T(8,128)S(1)}, u32[]{:S(2)}, u32[]{:S(2)}) collective-permute-start(f32[2,8,4096]{2,1,0:T(8,128)S(1)} %get-tuple-element.12), channel_id=1, source_target_pairs={{1,2},{2,1},{5,6},{6,5},{9,10},{10,9},{13,14},{14,13},{17,18},{18,... | collective-permute-start | bytes 786440 | tf_op jit(solution)/shard_map/ppermute | solution.py:229
  13.1 0.0 copy-done
  13.2 0.0 collective-permute-done
  13.2 4.3 %collective-permute-done.1 = f32[2,8,4096]{2,1,0:T(8,128)S(1)} collective-permute-done((f32[2,8,4096]{2,1,0:T(8,128)S(1)}, f32[2,8,4096]{2,1,0:T(8,128)S(1)}, u32[]{:S(2)}, u32[]{:S(2)}) %collective-permute-start.1) | collective-permute-done | bytes 262176 | tf_op jit(solution)/shard_map/ppermute | solution.py:229
  17.5 1.0 %pad_maximum_fusion = f32[4,2,8,4096]{3,2,1,0:T(8,128)} fusion(f32[2,2,8,4096]{3,2,1,0:T(8,128)S(1)} %copy_bitcast_fusion, f32[1,2,8,4096]{3,2,1,0:T(8,128)S(1)} %bitcast.25, f32[1,2,8,4096]{3,2,1,0:T(8,128)S(1)} %bitcast.23), kind=kLoop, calls=%fused_computation | loop fusion | flops 524288 | bytes 2097152 | tf_op jit(solution)/shard_map/concatenate | solution.py:260
  18.5 1.9 %collective-permute-start.3 = (f32[4,2,8,4096]{3,2,1,0:T(8,128)}, f32[4,2,8,4096]{3,2,1,0:T(8,128)S(1)}, u32[]{:S(2)}, u32[]{:S(2)}) collective-permute-start(f32[4,2,8,4096]{3,2,1,0:T(8,128)} %pad_maximum_fusion), channel_id=1, source_target_pairs={{0,4},{8,12},{16,20},{24,28},{32,36},{40,44},{48,52},{56,60},{64,6... | collective-permute-start | bytes 3145736 | tf_op jit(solution)/shard_map/ppermute | solution.py:229
  20.4 0.0 copy-start.1
  20.5 12.1 %collective-permute-start.2 = (f32[2,2,8,4096]{3,2,1,0:T(8,128)S(1)}, f32[2,2,8,4096]{3,2,1,0:T(8,128)S(1)}, u32[]{:S(2)}, u32[]{:S(2)}) collective-permute-start(f32[2,2,8,4096]{3,2,1,0:T(8,128)S(1)} %pad_maximum_fusion.1.mine_halo), channel_id=1, source_target_pairs={{4,8},{12,16},{20,24},{28,32},{36,40},{44,48},{52,56},{60,64},{68,... | collective-permute-start | bytes 1572872 | tf_op jit(solution)/shard_map/ppermute | solution.py:229
  32.6 1.9 %collective-permute-start.4 = (f32[2,16,4096]{2,1,0:T(8,128)S(1)}, f32[2,16,4096]{2,1,0:T(8,128)S(1)}, u32[]{:S(2)}, u32[]{:S(2)}) collective-permute-start(f32[2,16,4096]{2,1,0:T(8,128)S(1)} %copy-done), channel_id=1, source_target_pairs={{4,8},{12,16},{20,24},{28,32},{36,40},{44,48},{52,56},{60,64},{68,... | collective-permute-start | bytes 1572872 | tf_op jit(solution)/shard_map/ppermute | solution.py:229
  34.6 0.1 reshape.58
  34.7 0.1 add_convert_fusion.2.own_meta
  34.8 0.1 add_convert_fusion.edge_ref
  34.8 0.1 pad_add_fusion.place_ref
  34.9 4.6 %collective-permute-done.2.across_halo = f32[2,2,8,4096]{3,2,1,0:T(8,128)S(1)} collective-permute-done((f32[2,2,8,4096]{3,2,1,0:T(8,128)S(1)}, f32[2,2,8,4096]{3,2,1,0:T(8,128)S(1)}, u32[]{:S(2)}, u32[]{:S(2)}) %collective-permute-start.2) | collective-permute-done | bytes 524320 | tf_op jit(solution)/shard_map/ppermute | solution.py:229
  39.5 0.0 collective-permute-done.3.inside_all
  39.5 6.9 %collective-permute-done.4.across_mid = f32[2,16,4096]{2,1,0:T(8,128)S(1)} collective-permute-done((f32[2,16,4096]{2,1,0:T(8,128)S(1)}, f32[2,16,4096]{2,1,0:T(8,128)S(1)}, u32[]{:S(2)}, u32[]{:S(2)}) %collective-permute-start.4) | collective-permute-done | bytes 524320 | tf_op jit(solution)/shard_map/ppermute | solution.py:229
  46.5 0.0 copy-done.1
  46.5 10.6 %exchange.1 = (f32[2,16,4096]{2,1,0:T(8,128)S(1)}, f32[2,16,4096]{2,1,0:T(8,128)S(1)}, f32[2,16,4096]{2,1,0:T(8,128)S(1)}) custom-call(s32[3]{0:T(128)S(1)} %pad_add_fusion.place_ref, f32[12]{0:T(128)S(1)} %fusion.across_meta, f32[12]{0:T(128)S(1)} %add_convert_fusion.2.own_meta, f32[12]{0:T(128)S(1)} %fusion.1.inside_meta, f32[2]{0:T(128)S(1)} %add_convert_fusion.edge_ref, ...), custom_call_target="tpu_custom_call" | custom-call | flops 60000000 | bytes 5242880 | tf_op jit(solution)/shard_map/exchange/pallas_call | solution.py:274
  57.1 5.6 %collective-permute-start.5 = (f32[2,16,4096]{2,1,0:T(8,128)S(1)}, f32[2,16,4096]{2,1,0:T(8,128)S(1)}, u32[]{:S(2)}, u32[]{:S(2)}) collective-permute-start(f32[2,16,4096]{2,1,0:T(8,128)S(1)} %get-tuple-element.9), channel_id=1, source_target_pairs={{4,8},{12,16},{20,24},{28,32},{36,40},{44,48},{52,56},{60,64},{68,... | collective-permute-start | bytes 1572872 | tf_op jit(solution)/shard_map/ppermute | solution.py:229
  62.8 1.9 %collective-permute-start.6 = (f32[2,16,4096]{2,1,0:T(8,128)S(1)}, f32[2,16,4096]{2,1,0:T(8,128)S(1)}, u32[]{:S(2)}, u32[]{:S(2)}) collective-permute-start(f32[2,16,4096]{2,1,0:T(8,128)S(1)} %get-tuple-element.10), channel_id=1, source_target_pairs={{0,4},{8,12},{16,20},{24,28},{32,36},{40,44},{48,52},{56,60},{64,6... | collective-permute-start | bytes 1572872 | tf_op jit(solution)/shard_map/ppermute | solution.py:229
  64.7 6.2 %collective-permute-done.5 = f32[2,16,4096]{2,1,0:T(8,128)S(1)} collective-permute-done((f32[2,16,4096]{2,1,0:T(8,128)S(1)}, f32[2,16,4096]{2,1,0:T(8,128)S(1)}, u32[]{:S(2)}, u32[]{:S(2)}) %collective-permute-start.5) | collective-permute-done | bytes 524320 | tf_op jit(solution)/shard_map/ppermute | solution.py:229
  70.9 0.0 collective-permute-done.6
  70.9 0.9 %add_add_fusion = f32[2,16,4096]{2,1,0:T(8,128)} fusion(f32[2,16,4096]{2,1,0:T(8,128)S(1)} %collective-permute-done.6, f32[2,16,4096]{2,1,0:T(8,128)S(1)} %get-tuple-element.8, f32[2,16,4096]{2,1,0:T(8,128)S(1)} %collective-permute-done.5), kind=kLoop, calls=%fused_computation.3 | loop fusion | flops 262144 | bytes 2097152 | tf_op jit(solution)/shard_map/add | solution.py:295
  (4 shorter events, 0.1 us)
Async XLA Ops:
  0.0 0.7 copy-start.4
  0.8 0.7 copy-start.2
  0.8 0.7 copy-start.3
  1.5 11.6 %copy-start = (f32[2,16,4096]{2,1,0:T(8,128)S(1)}, f32[2,16,4096]{2,1,0:T(8,128)}, u32[]{:S(2)}) copy-start(f32[2,16,4096]{2,1,0:T(8,128)} %mine_mid.1) | copy-start | bytes 1572868
  2.9 10.3 %collective-permute-start = (f32[2,8,4096]{2,1,0:T(8,128)S(1)}, f32[2,8,4096]{2,1,0:T(8,128)S(1)}, u32[]{:S(2)}, u32[]{:S(2)}) collective-permute-start(f32[2,8,4096]{2,1,0:T(8,128)S(1)} %dynamic_update_slice.3), channel_id=1, source_target_pairs={{0,1},{2,3},{1,0},{3,2},{4,5},{6,7},{5,4},{7,6},{8,9},{10,11},{9,8... | collective-permute-start | bytes 786440 | tf_op jit(solution)/shard_map/ppermute | solution.py:229
  6.0 11.5 %collective-permute-start.1 = (f32[2,8,4096]{2,1,0:T(8,128)S(1)}, f32[2,8,4096]{2,1,0:T(8,128)S(1)}, u32[]{:S(2)}, u32[]{:S(2)}) collective-permute-start(f32[2,8,4096]{2,1,0:T(8,128)S(1)} %get-tuple-element.12), channel_id=1, source_target_pairs={{1,2},{2,1},{5,6},{6,5},{9,10},{10,9},{13,14},{14,13},{17,18},{18,... | collective-permute-start | bytes 786440 | tf_op jit(solution)/shard_map/ppermute | solution.py:229
  18.5 21.0 %collective-permute-start.3 = (f32[4,2,8,4096]{3,2,1,0:T(8,128)}, f32[4,2,8,4096]{3,2,1,0:T(8,128)S(1)}, u32[]{:S(2)}, u32[]{:S(2)}) collective-permute-start(f32[4,2,8,4096]{3,2,1,0:T(8,128)} %pad_maximum_fusion), channel_id=1, source_target_pairs={{0,4},{8,12},{16,20},{24,28},{32,36},{40,44},{48,52},{56,60},{64,6... | collective-permute-start | bytes 3145736 | tf_op jit(solution)/shard_map/ppermute | solution.py:229
  20.4 26.0 %copy-start.1 = (bf16[256,256]{1,0:T(8,128)(2,1)S(1)}, bf16[256,256]{1,0:T(8,128)(2,1)}, u32[]{:S(2)}) copy-start(bf16[256,256]{1,0:T(8,128)(2,1)} %constant.57.clone.table_ref) | copy-start | bytes 393220
  20.5 19.0 %collective-permute-start.2 = (f32[2,2,8,4096]{3,2,1,0:T(8,128)S(1)}, f32[2,2,8,4096]{3,2,1,0:T(8,128)S(1)}, u32[]{:S(2)}, u32[]{:S(2)}) collective-permute-start(f32[2,2,8,4096]{3,2,1,0:T(8,128)S(1)} %pad_maximum_fusion.1.mine_halo), channel_id=1, source_target_pairs={{4,8},{12,16},{20,24},{28,32},{36,40},{44,48},{52,56},{60,64},{68,... | collective-permute-start | bytes 1572872 | tf_op jit(solution)/shard_map/ppermute | solution.py:229
  32.6 13.8 %collective-permute-start.4 = (f32[2,16,4096]{2,1,0:T(8,128)S(1)}, f32[2,16,4096]{2,1,0:T(8,128)S(1)}, u32[]{:S(2)}, u32[]{:S(2)}) collective-permute-start(f32[2,16,4096]{2,1,0:T(8,128)S(1)} %copy-done), channel_id=1, source_target_pairs={{4,8},{12,16},{20,24},{28,32},{36,40},{44,48},{52,56},{60,64},{68,... | collective-permute-start | bytes 1572872 | tf_op jit(solution)/shard_map/ppermute | solution.py:229
  57.1 13.8 %collective-permute-start.5 = (f32[2,16,4096]{2,1,0:T(8,128)S(1)}, f32[2,16,4096]{2,1,0:T(8,128)S(1)}, u32[]{:S(2)}, u32[]{:S(2)}) collective-permute-start(f32[2,16,4096]{2,1,0:T(8,128)S(1)} %get-tuple-element.9), channel_id=1, source_target_pairs={{4,8},{12,16},{20,24},{28,32},{36,40},{44,48},{52,56},{60,64},{68,... | collective-permute-start | bytes 1572872 | tf_op jit(solution)/shard_map/ppermute | solution.py:229
  62.8 8.2 %collective-permute-start.6 = (f32[2,16,4096]{2,1,0:T(8,128)S(1)}, f32[2,16,4096]{2,1,0:T(8,128)S(1)}, u32[]{:S(2)}, u32[]{:S(2)}) collective-permute-start(f32[2,16,4096]{2,1,0:T(8,128)S(1)} %get-tuple-element.10), channel_id=1, source_target_pairs={{0,4},{8,12},{16,20},{24,28},{32,36},{40,44},{48,52},{56,60},{64,6... | collective-permute-start | bytes 1572872 | tf_op jit(solution)/shard_map/ppermute | solution.py:229

commit v3 on v2

--- a/solution.py
+++ b/solution.py
@@ -186,15 +186,11 @@
 
     lax.fori_loop(0, slots, pair_density, 0)
 
-    def two_sweeps(k, _):
-        weight = jnp.where(k == 0, coef[2] / coef[3], jnp.where(k == 1, coef[1] / coef[3], coef[0] / coef[3]))
+    for k in reversed(range(SWEEPS // 2 - 1)):
         for slot in range(slots):
             sweep(slot, None)
         for slot in range(slots):
-            sweep(slot, weight)
-        return 0
-
-    lax.fori_loop(0, SWEEPS // 2 - 1, two_sweeps, 0)
+            sweep(slot, coef[k] / coef[-1])
 
     def terms(slot, _):
         left, row, which, _, dy, dz = slot_scalars(slot, place_ref, metas)

time: 72.1 us -> 71.2 us (0.988)
  Pallas kernels: 10.6 us -> 9.73 us
    pallas_call x1, Pallas kernels: 10.6 us -> 9.73 us  [per_device(): pl.pallas_call(functools.partial(exchange_kernel, [float(g) for g in even...]
where the time goes in v3:
time: 71.2 us; the launch traced here: 70.9 us
  starting transfers between devices  33.8 us (47%)
  waiting for transfers between devices  22 us (31%)
  Pallas kernels  9.73 us (14%)
  local copies, waits for them, and re-layouts  2.93 us (4%)
  other arithmetic  2.26 us (3%)
    ppermute x7, starting transfers between devices, swapped(): return lax.ppermute(x, axis, pairs + [(b, a) for a, b in pairs])  33.8 us
    ppermute x7, waiting for transfers between devices, swapped(): return lax.ppermute(x, axis, pairs + [(b, a) for a, b in pairs])  22 us
    pallas_call x1, Pallas kernels, per_device(): pl.pallas_call(functools.partial(exchange_kernel, [float(g) for g in even...  9.73 us
  transfers between devices with their start and end apart: 7, of which 4 were waited for; matrix products, arithmetic and copies ran while one was open for 1% of the time, Pallas kernels for 0%

profile of v3, /device:TPU:4, one launch (start us, length us, event | category | flops | bytes accessed | tf_op | source)
XLA Modules:
  0.0 70.9 jit_solution(7224895394687136)
XLA Ops:
  0.0 0.0 copy-start.4
  0.0 0.7 copy-done.4
  0.7 0.1 concatenate.22
  0.8 0.0 copy-start.2
  0.8 0.0 copy-start.3
  0.8 0.7 copy-done.2
  1.4 0.0 copy-done.3
  1.4 0.1 add_convert_fusion.1
  1.5 0.0 copy-start
  1.5 1.1 %dynamic-slice_bitcast_fusion.1 = (f32[2,8,4096]{2,1,0:T(8,128)S(1)}, f32[2,8,4096]{2,1,0:T(8,128)S(1)}) fusion(f32[2,2,8,4096]{3,2,1,0:T(8,128)} %bitcast.22, s32[]{:T(128)S(6)} %select_n.32, s32[]{:T(128)S(6)} %select_n.34), kind=kLoop, calls=%fused_computation.5 | loop fusion | bytes 1048584 | tf_op jit(solution)/shard_map/jit(dynamic_index_in_dim)/squeeze | solution.py:246
  2.6 0.2 dynamic_update_slice.3
  2.9 3.1 %collective-permute-start = (f32[2,8,4096]{2,1,0:T(8,128)S(1)}, f32[2,8,4096]{2,1,0:T(8,128)S(1)}, u32[]{:S(2)}, u32[]{:S(2)}) collective-permute-start(f32[2,8,4096]{2,1,0:T(8,128)S(1)} %dynamic_update_slice.3), channel_id=1, source_target_pairs={{0,1},{2,3},{1,0},{3,2},{4,5},{6,7},{5,4},{7,6},{8,9},{10,11},{9,8... | collective-permute-start | bytes 786440 | tf_op jit(solution)/shard_map/ppermute | solution.py:225
  6.0 7.1 %collective-permute-start.1 = (f32[2,8,4096]{2,1,0:T(8,128)S(1)}, f32[2,8,4096]{2,1,0:T(8,128)S(1)}, u32[]{:S(2)}, u32[]{:S(2)}) collective-permute-start(f32[2,8,4096]{2,1,0:T(8,128)S(1)} %get-tuple-element.12), channel_id=1, source_target_pairs={{1,2},{2,1},{5,6},{6,5},{9,10},{10,9},{13,14},{14,13},{17,18},{18,... | collective-permute-start | bytes 786440 | tf_op jit(solution)/shard_map/ppermute | solution.py:225
  13.1 0.0 copy-done
  13.2 0.0 collective-permute-done
  13.2 4.3 %collective-permute-done.1 = f32[2,8,4096]{2,1,0:T(8,128)S(1)} collective-permute-done((f32[2,8,4096]{2,1,0:T(8,128)S(1)}, f32[2,8,4096]{2,1,0:T(8,128)S(1)}, u32[]{:S(2)}, u32[]{:S(2)}) %collective-permute-start.1) | collective-permute-done | bytes 262176 | tf_op jit(solution)/shard_map/ppermute | solution.py:225
  17.5 1.0 %pad_maximum_fusion = f32[4,2,8,4096]{3,2,1,0:T(8,128)} fusion(f32[2,2,8,4096]{3,2,1,0:T(8,128)S(1)} %copy_bitcast_fusion, f32[1,2,8,4096]{3,2,1,0:T(8,128)S(1)} %bitcast.25, f32[1,2,8,4096]{3,2,1,0:T(8,128)S(1)} %bitcast.23), kind=kLoop, calls=%fused_computation | loop fusion | flops 524288 | bytes 2097152 | tf_op jit(solution)/shard_map/concatenate | solution.py:256
  18.5 1.9 %collective-permute-start.3 = (f32[4,2,8,4096]{3,2,1,0:T(8,128)}, f32[4,2,8,4096]{3,2,1,0:T(8,128)S(1)}, u32[]{:S(2)}, u32[]{:S(2)}) collective-permute-start(f32[4,2,8,4096]{3,2,1,0:T(8,128)} %pad_maximum_fusion), channel_id=1, source_target_pairs={{0,4},{8,12},{16,20},{24,28},{32,36},{40,44},{48,52},{56,60},{64,6... | collective-permute-start | bytes 3145736 | tf_op jit(solution)/shard_map/ppermute | solution.py:225
  20.4 0.0 copy-start.1
  20.5 12.1 %collective-permute-start.2 = (f32[2,2,8,4096]{3,2,1,0:T(8,128)S(1)}, f32[2,2,8,4096]{3,2,1,0:T(8,128)S(1)}, u32[]{:S(2)}, u32[]{:S(2)}) collective-permute-start(f32[2,2,8,4096]{3,2,1,0:T(8,128)S(1)} %pad_maximum_fusion.1.mine_halo), channel_id=1, source_target_pairs={{4,8},{12,16},{20,24},{28,32},{36,40},{44,48},{52,56},{60,64},{68,... | collective-permute-start | bytes 1572872 | tf_op jit(solution)/shard_map/ppermute | solution.py:225
  32.6 1.9 %collective-permute-start.4 = (f32[2,16,4096]{2,1,0:T(8,128)S(1)}, f32[2,16,4096]{2,1,0:T(8,128)S(1)}, u32[]{:S(2)}, u32[]{:S(2)}) collective-permute-start(f32[2,16,4096]{2,1,0:T(8,128)S(1)} %copy-done), channel_id=1, source_target_pairs={{4,8},{12,16},{20,24},{28,32},{36,40},{44,48},{52,56},{60,64},{68,... | collective-permute-start | bytes 1572872 | tf_op jit(solution)/shard_map/ppermute | solution.py:225
  34.6 0.1 reshape.58
  34.7 0.1 add_convert_fusion.2.own_meta
  34.8 0.1 add_convert_fusion.edge_ref
  34.8 0.1 pad_add_fusion.place_ref
  34.9 4.6 %collective-permute-done.2.across_halo = f32[2,2,8,4096]{3,2,1,0:T(8,128)S(1)} collective-permute-done((f32[2,2,8,4096]{3,2,1,0:T(8,128)S(1)}, f32[2,2,8,4096]{3,2,1,0:T(8,128)S(1)}, u32[]{:S(2)}, u32[]{:S(2)}) %collective-permute-start.2) | collective-permute-done | bytes 524320 | tf_op jit(solution)/shard_map/ppermute | solution.py:225
  39.5 0.0 collective-permute-done.3.inside_all
  39.5 6.9 %collective-permute-done.4.across_mid = f32[2,16,4096]{2,1,0:T(8,128)S(1)} collective-permute-done((f32[2,16,4096]{2,1,0:T(8,128)S(1)}, f32[2,16,4096]{2,1,0:T(8,128)S(1)}, u32[]{:S(2)}, u32[]{:S(2)}) %collective-permute-start.4) | collective-permute-done | bytes 524320 | tf_op jit(solution)/shard_map/ppermute | solution.py:225
  46.5 0.0 copy-done.1
  46.5 9.7 %exchange.1 = (f32[2,16,4096]{2,1,0:T(8,128)S(1)}, f32[2,16,4096]{2,1,0:T(8,128)S(1)}, f32[2,16,4096]{2,1,0:T(8,128)S(1)}) custom-call(s32[3]{0:T(128)S(1)} %pad_add_fusion.place_ref, f32[12]{0:T(128)S(1)} %fusion.across_meta, f32[12]{0:T(128)S(1)} %add_convert_fusion.2.own_meta, f32[12]{0:T(128)S(1)} %fusion.1.inside_meta, f32[2]{0:T(128)S(1)} %add_convert_fusion.edge_ref, ...), custom_call_target="tpu_custom_call" | custom-call | flops 60000000 | bytes 5242880 | tf_op jit(solution)/shard_map/exchange/pallas_call | solution.py:270
  56.2 5.7 %collective-permute-start.5 = (f32[2,16,4096]{2,1,0:T(8,128)S(1)}, f32[2,16,4096]{2,1,0:T(8,128)S(1)}, u32[]{:S(2)}, u32[]{:S(2)}) collective-permute-start(f32[2,16,4096]{2,1,0:T(8,128)S(1)} %get-tuple-element.9), channel_id=1, source_target_pairs={{4,8},{12,16},{20,24},{28,32},{36,40},{44,48},{52,56},{60,64},{68,... | collective-permute-start | bytes 1572872 | tf_op jit(solution)/shard_map/ppermute | solution.py:225
  61.9 1.9 %collective-permute-start.6 = (f32[2,16,4096]{2,1,0:T(8,128)S(1)}, f32[2,16,4096]{2,1,0:T(8,128)S(1)}, u32[]{:S(2)}, u32[]{:S(2)}) collective-permute-start(f32[2,16,4096]{2,1,0:T(8,128)S(1)} %get-tuple-element.10), channel_id=1, source_target_pairs={{0,4},{8,12},{16,20},{24,28},{32,36},{40,44},{48,52},{56,60},{64,6... | collective-permute-start | bytes 1572872 | tf_op jit(solution)/shard_map/ppermute | solution.py:225
  63.8 6.2 %collective-permute-done.5 = f32[2,16,4096]{2,1,0:T(8,128)S(1)} collective-permute-done((f32[2,16,4096]{2,1,0:T(8,128)S(1)}, f32[2,16,4096]{2,1,0:T(8,128)S(1)}, u32[]{:S(2)}, u32[]{:S(2)}) %collective-permute-start.5) | collective-permute-done | bytes 524320 | tf_op jit(solution)/shard_map/ppermute | solution.py:225
  70.0 0.0 collective-permute-done.6
  70.0 0.9 %add_add_fusion = f32[2,16,4096]{2,1,0:T(8,128)} fusion(f32[2,16,4096]{2,1,0:T(8,128)S(1)} %collective-permute-done.6, f32[2,16,4096]{2,1,0:T(8,128)S(1)} %get-tuple-element.8, f32[2,16,4096]{2,1,0:T(8,128)S(1)} %collective-permute-done.5), kind=kLoop, calls=%fused_computation.3 | loop fusion | flops 262144 | bytes 2097152 | tf_op jit(solution)/shard_map/add | solution.py:291
  (4 shorter events, 0.1 us)
Async XLA Ops:
  0.0 0.7 copy-start.4
  0.8 0.7 copy-start.2
  0.8 0.7 copy-start.3
  1.5 11.6 %copy-start = (f32[2,16,4096]{2,1,0:T(8,128)S(1)}, f32[2,16,4096]{2,1,0:T(8,128)}, u32[]{:S(2)}) copy-start(f32[2,16,4096]{2,1,0:T(8,128)} %mine_mid.1) | copy-start | bytes 1572868
  2.9 10.3 %collective-permute-start = (f32[2,8,4096]{2,1,0:T(8,128)S(1)}, f32[2,8,4096]{2,1,0:T(8,128)S(1)}, u32[]{:S(2)}, u32[]{:S(2)}) collective-permute-start(f32[2,8,4096]{2,1,0:T(8,128)S(1)} %dynamic_update_slice.3), channel_id=1, source_target_pairs={{0,1},{2,3},{1,0},{3,2},{4,5},{6,7},{5,4},{7,6},{8,9},{10,11},{9,8... | collective-permute-start | bytes 786440 | tf_op jit(solution)/shard_map/ppermute | solution.py:225
  6.0 11.5 %collective-permute-start.1 = (f32[2,8,4096]{2,1,0:T(8,128)S(1)}, f32[2,8,4096]{2,1,0:T(8,128)S(1)}, u32[]{:S(2)}, u32[]{:S(2)}) collective-permute-start(f32[2,8,4096]{2,1,0:T(8,128)S(1)} %get-tuple-element.12), channel_id=1, source_target_pairs={{1,2},{2,1},{5,6},{6,5},{9,10},{10,9},{13,14},{14,13},{17,18},{18,... | collective-permute-start | bytes 786440 | tf_op jit(solution)/shard_map/ppermute | solution.py:225
  18.5 21.0 %collective-permute-start.3 = (f32[4,2,8,4096]{3,2,1,0:T(8,128)}, f32[4,2,8,4096]{3,2,1,0:T(8,128)S(1)}, u32[]{:S(2)}, u32[]{:S(2)}) collective-permute-start(f32[4,2,8,4096]{3,2,1,0:T(8,128)} %pad_maximum_fusion), channel_id=1, source_target_pairs={{0,4},{8,12},{16,20},{24,28},{32,36},{40,44},{48,52},{56,60},{64,6... | collective-permute-start | bytes 3145736 | tf_op jit(solution)/shard_map/ppermute | solution.py:225
  20.4 26.0 %copy-start.1 = (bf16[256,256]{1,0:T(8,128)(2,1)S(1)}, bf16[256,256]{1,0:T(8,128)(2,1)}, u32[]{:S(2)}) copy-start(bf16[256,256]{1,0:T(8,128)(2,1)} %constant.57.clone.table_ref) | copy-start | bytes 393220
  20.5 19.0 %collective-permute-start.2 = (f32[2,2,8,4096]{3,2,1,0:T(8,128)S(1)}, f32[2,2,8,4096]{3,2,1,0:T(8,128)S(1)}, u32[]{:S(2)}, u32[]{:S(2)}) collective-permute-start(f32[2,2,8,4096]{3,2,1,0:T(8,128)S(1)} %pad_maximum_fusion.1.mine_halo), channel_id=1, source_target_pairs={{4,8},{12,16},{20,24},{28,32},{36,40},{44,48},{52,56},{60,64},{68,... | collective-permute-start | bytes 1572872 | tf_op jit(solution)/shard_map/ppermute | solution.py:225
  32.6 13.8 %collective-permute-start.4 = (f32[2,16,4096]{2,1,0:T(8,128)S(1)}, f32[2,16,4096]{2,1,0:T(8,128)S(1)}, u32[]{:S(2)}, u32[]{:S(2)}) collective-permute-start(f32[2,16,4096]{2,1,0:T(8,128)S(1)} %copy-done), channel_id=1, source_target_pairs={{4,8},{12,16},{20,24},{28,32},{36,40},{44,48},{52,56},{60,64},{68,... | collective-permute-start | bytes 1572872 | tf_op jit(solution)/shard_map/ppermute | solution.py:225
  56.2 13.8 %collective-permute-start.5 = (f32[2,16,4096]{2,1,0:T(8,128)S(1)}, f32[2,16,4096]{2,1,0:T(8,128)S(1)}, u32[]{:S(2)}, u32[]{:S(2)}) collective-permute-start(f32[2,16,4096]{2,1,0:T(8,128)S(1)} %get-tuple-element.9), channel_id=1, source_target_pairs={{4,8},{12,16},{20,24},{28,32},{36,40},{44,48},{52,56},{60,64},{68,... | collective-permute-start | bytes 1572872 | tf_op jit(solution)/shard_map/ppermute | solution.py:225
  61.9 8.2 %collective-permute-start.6 = (f32[2,16,4096]{2,1,0:T(8,128)S(1)}, f32[2,16,4096]{2,1,0:T(8,128)S(1)}, u32[]{:S(2)}, u32[]{:S(2)}) collective-permute-start(f32[2,16,4096]{2,1,0:T(8,128)S(1)} %get-tuple-element.10), channel_id=1, source_target_pairs={{0,4},{8,12},{16,20},{24,28},{32,36},{40,44},{48,52},{56,60},{64,6... | collective-permute-start | bytes 1572872 | tf_op jit(solution)/shard_map/ppermute | solution.py:225
